TPU v7x, 32 devices: a whole 2x2x4 slice. The times are simulated.
32 devices in a mesh: wave: 4 (over y, x), freq: 8 (over z, core).
Axes of the slice: x: 2, y: 2, z: 4, core: 2. Of those that a mesh axis runs over, the one named last changes fastest.
Arguments:
- waveforms: float32 [1024, 16384], P('wave', 'freq'), may hold values from -6 to 6
- pivots: int32 [2, 128], replicated, may hold values from 0 to 1023, as said below
- nodes: int32 [1024], replicated, may hold values from 0 to 16383, as said below
Outputs:
- residual: float32 [1024, 16384], P('wave', 'freq')
- basis_rows: float32 [256, 16384], P(None, 'freq')
- fitted: float32 [1024, 16384], P('wave', 'freq')
Inputs may be any that keep to these rules, and one draw needn't show every extreme that they name: `pivots`: all 256 pivot indices are different. `nodes`: all node indices are different.
All inputs are finite; a program needn't handle non-finite values.
Results may differ from a plain program's by a relative error of at most 0.0001.
Values sent between devices are 32-bit elements; how exact they have to be, the bound alone decides.
A program may use at most 64 MiB of HBM per device.

v0:
```python
import jax
import jax.numpy as jnp
from jax import lax
from jax.sharding import PartitionSpec as P

HIGH = lax.Precision.HIGH


def body(waveforms, pivots, nodes):
    rows_here, cols_here = waveforms.shape
    row_start = lax.axis_index("wave") * rows_here
    col_start = lax.axis_index("freq") * cols_here
    picks = pivots.reshape(-1)
    count = picks.shape[0]
    local_rows = picks - row_start
    inside = ((local_rows >= 0) & (local_rows < rows_here)).astype(jnp.float32)
    picked = jnp.take(waveforms, jnp.clip(local_rows, 0, rows_here - 1), axis=0) * inside[:, None]
    pivot_rows = lax.psum(picked, "wave")
    columns = col_start + jnp.arange(cols_here, dtype=jnp.int32)
    node_count = jnp.sum((nodes[:, None] == columns[None, :]).astype(jnp.float32), axis=0)
    weighted = pivot_rows * node_count[None, :]
    left = jnp.concatenate([pivot_rows, waveforms], axis=0)
    right = jnp.concatenate([pivot_rows, weighted], axis=0)
    total = lax.psum(jnp.dot(left, right.T, precision=HIGH), "freq")
    gram, node_gram = (total[:count, :count], total[:count, count:])
    cross, node_cross = (total[count:, :count], total[count:, count:])
    factors = jnp.linalg.cholesky(jnp.stack([gram, node_gram]))
    eye = jnp.broadcast_to(jnp.eye(count, dtype=jnp.float32), factors.shape)
    inverses = jax.scipy.linalg.solve_triangular(factors, eye, lower=True)
    hi = lax.Precision.HIGHEST
    basis_rows = jnp.dot(inverses[0], pivot_rows, precision=HIGH)
    coeffs = jnp.dot(cross, inverses[0].T, precision=hi)
    residual = waveforms - jnp.dot(coeffs, basis_rows, precision=HIGH)
    coefficients = jnp.dot(
        jnp.dot(node_cross, inverses[1].T, precision=hi), inverses[1], precision=hi
    )
    fitted = jnp.dot(coefficients, pivot_rows, precision=HIGH)
    return (residual, basis_rows, fitted)


def solution(mesh):
    in_specs = (P("wave", "freq"), P(), P())
    out_specs = (P("wave", "freq"), P(None, "freq"), P("wave", "freq"))
    return jax.shard_map(body, mesh=mesh, in_specs=in_specs, out_specs=out_specs, check_vma=False)
```

profile of v0, /device:TPU:0, one launch (start us, length us, event | category | flops | bytes accessed | tf_op | source)
XLA Modules:
  0.0 288.0 jit_solution(7392579073697744297)
XLA Ops:
  7.2 0.0 all-reduce.4.cloned.1.call-start
  7.2 0.7 fusion.25
  7.9 0.7 compare_and_fusion
  8.6 4.0 %gather_fusion = f32[256,2048]{1,0:T(8,128)S(1)} fusion(f32[256,2048]{1,0:T(8,128)} %param.3, s32[1024]{0:T(1024)S(1)} %pad_clamp_fusion), kind=kCustom, calls=%fused_computation | custom fusion | bytes 4195328 | tf_op jit(solution)/shard_map/jit(_take)/gather | solution.py:17
  12.6 1.6 select_multiply_fusion
  14.2 0.0 copy-start.6
  14.2 0.0 all-reduce.4.cloned.1.call-update
  14.2 0.0 all-reduce.6.cloned.1.call-start
  14.3 0.5 copy-done.6
  14.9 0.9 convert_reduce_fusion
  15.8 0.0 copy-start
  15.8 70.8 %all-reduce.4.cloned.1.call-done = f32[256,2048]{1,0:T(8,128)} async-done(((f32[256,2048]{1,0:T(8,128)}), f32[256,2048]{1,0:T(8,128)}) %all-reduce.4.cloned.1.call-update) | async-done | bytes 2097168 | tf_op jit(solution)/shard_map/psum | solution.py:18
  86.6 0.0 copy-start.1
  86.6 2.0 broadcast_multiply_fusion
  88.5 0.0 copy-done
  88.6 0.2 copy-done.1
  88.8 4.6 %fusion = f32[512,512]{0,1:T(8,128)} fusion(f32[256,2048]{1,0:T(8,128)S(1)} %copy-done.1, f32[256,2048]{1,0:T(8,128)S(1)} %copy-done, f32[256,2048]{1,0:T(8,128)S(1)} %broadcast_multiply_fusion), kind=kOutput, calls=%fused_computation.6 | convolution fusion | flops 3223322624 | bytes 7340032 | tf_op jit(solution)/shard_map/dot_general | solution.py:24
  93.4 0.0 all-reduce.6.cloned.1.call-update
  93.5 59.4 %all-reduce.6.cloned.1.call-done = f32[512,512]{0,1:T(8,128)} async-done(((f32[512,512]{0,1:T(8,128)}), f32[512,512]{0,1:T(8,128)}) %all-reduce.6.cloned.1.call-update) | async-done | bytes 1048592 | tf_op jit(solution)/shard_map/psum | solution.py:24
  152.9 1.1 slice_bitcast_fusion.1
  153.9 0.8 pad_maximum_fusion.4
  154.8 1.2 copy.14
  156.0 0.1 fusion.3
  156.1 0.0 copy-start.4
  156.1 0.8 copy-done.4
  156.9 23.6 %custom-call.17 = f32[2,128,128]{2,1,0:T(8,128)S(1)} custom-call(f32[2,128,128]{2,1,0:T(8,128)S(1)} %cholesky.122), custom_call_target="Cholesky" | custom-call | tf_op jit(solution)/shard_map/jit(cholesky)/cholesky | solution.py:27
  180.6 19.7 %custom-call.18 = f32[2,1,128,128]{2,3,1,0:T(8,128)S(1)} custom-call(f32[2,1,128,128]{3,2,1,0:T(8,128)S(1)} %select_bitcast_fusion), custom_call_target="InvertDiagBlocksLowerTriangular" | custom-call | tf_op jit(solution)/shard_map/jit(cholesky)/cholesky | solution.py:27
  200.3 1.2 constant_dynamic-update-slice_fusion.1
  201.5 1.3 convolution_subtract_fusion.2
  202.8 23.5 %custom-call.19 = f32[2,128,128]{2,1,0:T(8,128)S(1)} custom-call(f32[2,128,128]{2,1,0:T(8,128)S(1)} %convolution_subtract_fusion.2), custom_call_target="Cholesky" | custom-call | tf_op jit(solution)/shard_map/jit(cholesky)/cholesky | solution.py:27
  226.3 0.2 compare_reduce_fusion
  226.4 0.1 select_select_fusion
  226.6 0.1 triangular_solve.66
  226.7 5.3 %while.1 = (s32[]{:T(128)}, f32[2,256,256]{2,1,0:T(8,128)S(1)}, s32[2,2]{1,0:T(2,128)S(1)}, f32[2,2,128,128]{3,2,0,1:T(8,128)}, s32[]{:T(128)}) while((s32[]{:T(128)}, f32[2,256,256]{2,1,0:T(8,128)S(1)}, s32[2,2]{1,0:T(2,128)S(1)}, f32[2,2,128,128]{3,2,0,1:T(8,128)}, s32[]{:T(128)}) %tuple.30), condition=%wide.while_cond, body=%wide.while_body.sunk | while | flops 2 | bytes 263277 | solution.py:29
  226.7 0.6 fusion.45
  227.3 2.0 bitcast_dynamic-update-slice_fusion.2
  229.3 0.6 fusion.45
  229.9 2.0 bitcast_dynamic-update-slice_fusion.2
  231.9 40.1 %custom-call.20 = f32[2,2,128,128]{2,3,1,0:T(8,128)S(1)} custom-call(f32[2,2,128,128]{3,2,1,0:T(8,128)} %bitcast.62), custom_call_target="InvertDiagBlocksLowerTriangular" | custom-call | tf_op jit(solution)/shard_map/jit(_solve_triangular)/vmap()/triangular_solve | solution.py:29
  272.1 0.0 copy-start.5
  272.1 0.4 fusion.14
  272.5 0.4 convolution_subtract_fusion.1
  272.9 0.0 copy-start.2
  272.9 0.4 fusion.13
  273.3 0.0 copy-done.5
  273.3 0.6 fusion.7
  273.9 0.4 fusion.19
  274.3 0.6 fusion.9
  274.9 0.0 copy-done.2
  274.9 1.2 fusion.22
  276.1 0.0 copy-start.3
  276.1 2.5 convolution_subtract_fusion
  278.7 0.0 copy-done.3
  278.7 2.5 fusion.33
  (17 shorter events, 0.2 us)
Async XLA Ops:
  7.2 79.4 %all-reduce.4.cloned.1.call-start = ((), (), s32[]{:S(2)}) async-start(), calls=%async_computation | async-start | bytes 4194304 | tf_op jit(solution)/shard_map/psum | solution.py:18
  14.2 0.7 copy-start.6
  14.2 138.6 %all-reduce.6.cloned.1.call-start = ((), (), s32[]{:S(2)}) async-start(), calls=%async_computation.1 | async-start | bytes 2097152 | tf_op jit(solution)/shard_map/psum | solution.py:24
  15.8 72.8 %copy-start = (f32[256,2048]{1,0:T(8,128)S(1)}, f32[256,2048]{1,0:T(8,128)}, u32[]{:S(2)}) copy-start(f32[256,2048]{1,0:T(8,128)} %param.3) | copy-start | bytes 6291460
  86.6 2.2 copy-start.1
  156.1 0.8 copy-start.4
  272.1 1.3 copy-start.5
  272.9 2.0 copy-start.2
  276.1 2.5 copy-start.3
Sparse Core Ops, SparseCore 0:
  14.3 72.1 all-reduce.3
  93.5 59.2 all-reduce.5
where the time goes:
time: 288 us
  waiting for transfers between devices  130 us (45%)
  other arithmetic  114 us (40%)
  matrix products  16.1 us (6%)
  between operations  14.3 us (5%)
  local copies, waits for them, and re-layouts  13.3 us (5%)
    psum x1, waiting for transfers between devices, body(): pivot_rows = lax.psum(picked, 'wave')  70.8 us
    another operation x10, other arithmetic, body(): factors = jnp.linalg.cholesky(jnp.stack([gram, node_gram]))  67.8 us
    psum x1, waiting for transfers between devices, body(): total = lax.psum(jnp.dot(left, right.T, precision=HIGH), 'freq')  59.4 us
    another operation x4, other arithmetic, body(): inverses = jax.scipy.linalg.solve_triangular(factors, eye, lower=True)  40.3 us
  transfers between devices with their start and end apart: 2, of which 2 were waited for; matrix products, arithmetic and copies ran while one was open for 0% of the time, Pallas kernels for 0%

commit v1 on v0

--- a/solution.py
+++ b/solution.py
@@ -15,7 +15,11 @@
     local_rows = picks - row_start
     inside = ((local_rows >= 0) & (local_rows < rows_here)).astype(jnp.float32)
     picked = jnp.take(waveforms, jnp.clip(local_rows, 0, rows_here - 1), axis=0) * inside[:, None]
-    pivot_rows = lax.psum(picked, "wave")
+    pivot_rows = picked
+    for hop in (1, 2):
+        pivot_rows = pivot_rows + lax.ppermute(
+            pivot_rows, "wave", [(dev, dev ^ hop) for dev in range(4)]
+        )
     columns = col_start + jnp.arange(cols_here, dtype=jnp.int32)
     node_count = jnp.sum((nodes[:, None] == columns[None, :]).astype(jnp.float32), axis=0)
     weighted = pivot_rows * node_count[None, :]

time: 288 us -> 317 us (1.10)
  waiting for transfers between devices: 130 us -> 151 us
  starting transfers between devices: 0.08 us -> 4.84 us
    ppermute x0 -> x2, waiting for transfers between devices: none -> 90 us  [body(): lax.ppermute(pivot_rows, 'wave', [(dev, dev ^ hop) for dev in range(4)])]
    psum x1 -> x0, waiting for transfers between devices: 70.8 us -> none  [body(): pivot_rows = lax.psum(picked, 'wave')]
    ppermute x0 -> x2, starting transfers between devices: none -> 4.8 us  [body(): lax.ppermute(pivot_rows, 'wave', [(dev, dev ^ hop) for dev in range(4)])]
  transfers between devices with their start and end apart: 2 -> 3, of which waited for: 2 -> 3; matrix products, arithmetic and copies ran while one was open for 0% -> 0% of each run, Pallas kernels for 0% -> 0%
where the time goes in v1:
time: 317 us; the launch traced here: 316 us
  waiting for transfers between devices  151 us (48%)
  other arithmetic  115 us (36%)
  matrix products  17.7 us (6%)
  between operations  14.3 us (5%)
  local copies, waits for them, and re-layouts  13.7 us (4%)
  starting transfers between devices  4.84 us (2%)
    ppermute x2, waiting for transfers between devices, body(): lax.ppermute(pivot_rows, 'wave', [(dev, dev ^ hop) for dev in range(4)])  90 us
    another operation x10, other arithmetic, body(): factors = jnp.linalg.cholesky(jnp.stack([gram, node_gram]))  67.8 us
    psum x1, waiting for transfers between devices, body(): total = lax.psum(jnp.dot(left, right.T, precision=HIGH), 'freq')  60.6 us
    another operation x4, other arithmetic, body(): inverses = jax.scipy.linalg.solve_triangular(factors, eye, lower=True)  40.3 us
  transfers between devices with their start and end apart: 3, of which 3 were waited for; matrix products, arithmetic and copies ran while one was open for 0% of the time, Pallas kernels for 0%

profile of v1, /device:TPU:0, one launch (start us, length us, event | category | flops | bytes accessed | tf_op | source)
XLA Modules:
  0.0 316.3 jit_solution(12016853093428532498)
XLA Ops:
  7.2 0.0 all-reduce.3.cloned.1.call-start
  7.2 0.7 fusion.25
  7.9 0.7 compare_and_fusion
  8.6 4.0 %gather_fusion = f32[256,2048]{1,0:T(8,128)S(1)} fusion(f32[256,2048]{1,0:T(8,128)} %param.3, s32[1024]{0:T(1024)S(1)} %pad_clamp_fusion), kind=kCustom, calls=%fused_computation | custom fusion | bytes 4195328 | tf_op jit(solution)/shard_map/jit(_take)/gather | solution.py:17
  12.6 0.3 select_multiply_fusion
  12.9 0.0 copy-start.6
  12.9 3.0 collective-permute-start
  15.9 45.6 %collective-permute-done = f32[256,2048]{1,0:T(8,128)S(1)} collective-permute-done((f32[256,2048]{1,0:T(8,128)S(1)}, f32[256,2048]{1,0:T(8,128)S(1)}, u32[]{:S(2)}, u32[]{:S(2)}) %collective-permute-start) | collective-permute-done | bytes 2097184 | tf_op jit(solution)/shard_map/ppermute | solution.py:20
  61.6 1.7 fusion.44
  63.3 1.8 collective-permute-start.1
  65.1 0.0 copy-done.6
  65.1 0.9 convert_reduce_fusion
  66.0 0.0 copy-start
  66.0 44.4 %collective-permute-done.1 = f32[256,2048]{1,0:T(8,128)} collective-permute-done((f32[256,2048]{1,0:T(8,128)}, f32[256,2048]{1,0:T(8,128)}, u32[]{:S(2)}, u32[]{:S(2)}) %collective-permute-start.1) | collective-permute-done | bytes 2097184 | tf_op jit(solution)/shard_map/ppermute | solution.py:20
  110.4 2.7 broadcast_multiply_fusion
  113.1 0.0 copy-start.1
  113.1 1.3 copy-done.1
  114.4 0.0 copy-done
  114.4 4.6 %fusion = f32[512,512]{0,1:T(8,128)} fusion(f32[256,2048]{1,0:T(8,128)S(1)} %get-tuple-element.22, f32[256,2048]{1,0:T(8,128)S(1)} %copy-done, f32[256,2048]{1,0:T(8,128)S(1)} %get-tuple-element.21), kind=kOutput, calls=%fused_computation.6 | convolution fusion | flops 3223322624 | bytes 7340032 | tf_op jit(solution)/shard_map/dot_general | solution.py:28
  119.0 0.0 all-reduce.3.cloned.1.call-update
  119.1 60.6 %all-reduce.3.cloned.1.call-done = f32[512,512]{0,1:T(8,128)} async-done(((f32[512,512]{0,1:T(8,128)}), f32[512,512]{0,1:T(8,128)}) %all-reduce.3.cloned.1.call-update) | async-done | bytes 1048592 | tf_op jit(solution)/shard_map/psum | solution.py:28
  179.7 1.1 slice_bitcast_fusion.1
  180.7 0.8 pad_maximum_fusion.4
  181.6 1.2 copy.14
  182.8 0.1 fusion.3
  182.9 0.0 copy-start.4
  182.9 0.8 copy-done.4
  183.7 23.6 %custom-call.17 = f32[2,128,128]{2,1,0:T(8,128)S(1)} custom-call(f32[2,128,128]{2,1,0:T(8,128)S(1)} %cholesky.122), custom_call_target="Cholesky" | custom-call | tf_op jit(solution)/shard_map/jit(cholesky)/cholesky | solution.py:31
  207.4 19.7 %custom-call.18 = f32[2,1,128,128]{2,3,1,0:T(8,128)S(1)} custom-call(f32[2,1,128,128]{3,2,1,0:T(8,128)S(1)} %select_bitcast_fusion), custom_call_target="InvertDiagBlocksLowerTriangular" | custom-call | tf_op jit(solution)/shard_map/jit(cholesky)/cholesky | solution.py:31
  227.1 1.2 constant_dynamic-update-slice_fusion.1
  228.3 1.3 convolution_subtract_fusion.2
  229.6 23.5 %custom-call.19 = f32[2,128,128]{2,1,0:T(8,128)S(1)} custom-call(f32[2,128,128]{2,1,0:T(8,128)S(1)} %convolution_subtract_fusion.2), custom_call_target="Cholesky" | custom-call | tf_op jit(solution)/shard_map/jit(cholesky)/cholesky | solution.py:31
  253.1 0.2 compare_reduce_fusion
  253.3 0.1 select_select_fusion
  253.4 0.1 triangular_solve.66
  253.5 5.2 %while.1 = (s32[]{:T(128)}, f32[2,256,256]{2,1,0:T(8,128)S(1)}, s32[2,2]{1,0:T(2,128)S(1)}, f32[2,2,128,128]{3,2,0,1:T(8,128)}, s32[]{:T(128)}) while((s32[]{:T(128)}, f32[2,256,256]{2,1,0:T(8,128)S(1)}, s32[2,2]{1,0:T(2,128)S(1)}, f32[2,2,128,128]{3,2,0,1:T(8,128)}, s32[]{:T(128)}) %tuple.31), condition=%wide.while_cond, body=%wide.while_body.sunk | while | flops 2 | bytes 263277 | solution.py:33
  253.5 0.6 fusion.46
  254.1 2.0 bitcast_dynamic-update-slice_fusion.2
  256.1 0.6 fusion.46
  256.6 2.0 bitcast_dynamic-update-slice_fusion.2
  258.6 40.1 %custom-call.20 = f32[2,2,128,128]{2,3,1,0:T(8,128)S(1)} custom-call(f32[2,2,128,128]{3,2,1,0:T(8,128)} %bitcast.62), custom_call_target="InvertDiagBlocksLowerTriangular" | custom-call | tf_op jit(solution)/shard_map/jit(_solve_triangular)/vmap()/triangular_solve | solution.py:33
  298.8 0.4 fusion.14
  299.2 0.4 convolution_subtract_fusion.1
  299.6 0.4 fusion.13
  300.0 0.0 copy-start.5
  300.0 0.0 copy-start.2
  300.0 2.8 fusion.22
  302.8 0.0 copy-done.5
  302.8 0.0 copy-start.3
  302.8 0.6 fusion.7
  303.4 0.4 fusion.19
  303.8 0.0 copy-done.2
  303.8 2.5 fusion.33
  306.3 0.6 fusion.9
  306.9 0.0 copy-done.3
  307.0 2.5 convolution_subtract_fusion
  (17 shorter events, 0.2 us)
Async XLA Ops:
  7.2 172.5 %all-reduce.3.cloned.1.call-start = ((), (), s32[]{:S(2)}) async-start(), calls=%async_computation | async-start | bytes 2097152 | tf_op jit(solution)/shard_map/psum | solution.py:28
  12.9 52.2 %copy-start.6 = (s32[1024]{0:T(1024)S(1)}, s32[1024]{0:T(1024)}, u32[]{:S(2)}) copy-start(s32[1024]{0:T(1024)} %param.5) | copy-start | bytes 12292
  12.9 48.7 %collective-permute-start = (f32[256,2048]{1,0:T(8,128)S(1)}, f32[256,2048]{1,0:T(8,128)S(1)}, u32[]{:S(2)}, u32[]{:S(2)}) collective-permute-start(f32[256,2048]{1,0:T(8,128)S(1)} %select_multiply_fusion), channel_id=1, source_target_pairs={{0,8},{8,0},{16,24},{24,16},{1,9},{9,1},{17,25},{25,17},{2,10},{10... | collective-permute-start | bytes 6291464 | tf_op jit(solution)/shard_map/ppermute | solution.py:20
  63.3 47.1 %collective-permute-start.1 = (f32[256,2048]{1,0:T(8,128)}, f32[256,2048]{1,0:T(8,128)}, u32[]{:S(2)}, u32[]{:S(2)}) collective-permute-start(f32[256,2048]{1,0:T(8,128)} %fusion.44), channel_id=1, source_target_pairs={{0,16},{8,24},{16,0},{24,8},{1,17},{9,25},{17,1},{25,9},{2,18},{10... | collective-permute-start | bytes 6291464 | tf_op jit(solution)/shard_map/ppermute | solution.py:20
  66.0 48.4 %copy-start = (f32[256,2048]{1,0:T(8,128)S(1)}, f32[256,2048]{1,0:T(8,128)}, u32[]{:S(2)}) copy-start(f32[256,2048]{1,0:T(8,128)} %param.3) | copy-start | bytes 6291460
  113.1 1.3 copy-start.1
  182.9 0.8 copy-start.4
  300.0 2.8 copy-start.5
  300.0 3.8 %copy-start.2 = (f32[256,2048]{1,0:T(8,128)S(1)}, f32[256,2048]{1,0:T(8,128)}, u32[]{:S(2)}) copy-start(f32[256,2048]{1,0:T(8,128)} %copy-done.1) | copy-start | bytes 6291460
  302.8 4.1 %copy-start.3 = (f32[256,2048]{1,0:T(8,128)}, f32[256,2048]{1,0:T(8,128)S(1)}, u32[]{:S(2)}) copy-start(f32[256,2048]{1,0:T(8,128)S(1)} %fusion.22) | copy-start | bytes 6291460
Sparse Core Ops, SparseCore 0:
  119.1 60.5 all-reduce.2
